TPU v7x, 256 devices: a whole 4x4x8 slice. The times are simulated.
256 devices in a mesh: ctx: 32 (over z, y), head: 8 (over x, core).
Axes of the slice: x: 4, y: 4, z: 8, core: 2. Of those that a mesh axis runs over, the one named last changes fastest.
Arguments:
- query_input: bfloat16 [16384, 4096], P(('ctx', 'head')), may hold values from -6 to 6
- key_input: bfloat16 [16384, 4096], P(('ctx', 'head')), may hold values from -6 to 6
- value_input: bfloat16 [16384, 4096], P(('ctx', 'head')), may hold values from -6 to 6
- cotangent: bfloat16 [16384, 4096], P(('ctx', 'head')), may hold values from -6 to 6
- level_codes: int32 [32, 15, 16384], P('head', None, 'ctx'), may hold values from 0 to 15
Outputs:
- attended: bfloat16 [16384, 4096], P(('ctx', 'head'))
- grad_queries: bfloat16 [16384, 4096], P(('ctx', 'head'))
- grad_keys: bfloat16 [16384, 4096], P(('ctx', 'head'))
- grad_values: bfloat16 [16384, 4096], P(('ctx', 'head'))
All inputs are finite; a program needn't handle non-finite values.
Results may differ from a plain program's by a relative error of at most 0.0074.
Values may be sent and summed in bfloat16 or wider, within the bound.
A program may use at most 128 MiB of HBM per device.

v0:
```python
import jax
import jax.numpy as jnp
from jax import lax
from jax.sharding import PartitionSpec as P


def swapped(block, axis, stride):
    count = lax.axis_size(axis)
    route = []
    for low in range(count):
        high = low | 1 << stride
        if high != low and high < count:
            route += [(low, high), (high, low)]
    return lax.ppermute(block, axis, route)


def for_sending(x):

    def short(part):
        return part.astype(jnp.bfloat16) if part.dtype == jnp.float32 else part

    return jax.tree.map(short, x)


def level_gain(level):
    if level == 0:
        return 1.0
    return 2.0 ** (-(level - 1) / 2.0)


def on_device(query_input, key_input, value_input, cotangent, level_codes):
    query_rows, key_rows, value_rows, cot_rows = (
        lax.all_to_all(query_input, "head", split_axis=1, concat_axis=0, tiled=True),
        lax.all_to_all(key_input, "head", split_axis=1, concat_axis=0, tiled=True),
        lax.all_to_all(value_input, "head", split_axis=1, concat_axis=0, tiled=True),
        lax.all_to_all(cotangent, "head", split_axis=1, concat_axis=0, tiled=True),
    )
    head_count = level_codes.shape[0]
    total_levels = level_codes.shape[1]
    length = query_rows.shape[0]
    head_dim = query_rows.shape[1] // head_count
    tok_bits = length.bit_length() - 1
    ctx_bits = total_levels - tok_bits - 1
    score_scale = head_dim ** (-0.5)
    head_shape = (length, head_count, head_dim)
    query_heads = query_rows.reshape(head_shape)
    key_heads = key_rows.reshape(head_shape)
    value_heads = value_rows.reshape(head_shape)
    cot_heads = cot_rows.reshape(head_shape)
    code_weights = level_codes.astype(jnp.float32) / 8.0
    my_block = lax.axis_index("ctx")
    cross_scale = jnp.stack(
        [
            code_weights[:, tok_bits + 1 + bit_index, :]
            * (score_scale * level_gain(tok_bits + 1 + bit_index))
            * (my_block // 2**bit_index % 2).astype(jnp.float32)
            for bit_index in range(ctx_bits)
        ]
    )
    row_scale = jnp.transpose(cross_scale, (0, 2, 1))
    block_state = jnp.einsum(
        "phd,phe->hde", key_heads, value_heads, preferred_element_type=jnp.float32
    )
    scaled_cot = (row_scale[..., None] * cot_heads[None]).astype(jnp.bfloat16)
    grad_state = jnp.einsum(
        "phd,bphe->bhde", query_heads, scaled_cot, preferred_element_type=jnp.float32
    )
    running = block_state
    bucket_list = []
    for bit_index in range(ctx_bits):
        partner = swapped(running.astype(jnp.bfloat16), "ctx", bit_index).astype(running.dtype)
        bit_set = (my_block // 2**bit_index % 2).astype(jnp.float32)
        bucket_list.append(bit_set * partner)
        running = running + partner
    bucket_sums = jnp.stack(bucket_list)
    bucket = bucket_sums.astype(jnp.bfloat16)
    carried = [grad_state[level_index] for level_index in range(ctx_bits)]
    pulled = jnp.zeros((head_count, head_dim, head_dim), jnp.float32)
    for bit_index in range(ctx_bits):
        partner = swapped(for_sending(jnp.stack(carried)), "ctx", bit_index)
        bit_clear = 1.0 - (my_block // 2**bit_index % 2).astype(jnp.float32)
        pulled = pulled + bit_clear * partner[0]
        carried = [
            carried[level_index + 1] + partner[level_index + 1]
            for level_index in range(len(carried) - 1)
        ]
    pulled_half = pulled.astype(jnp.bfloat16)
    block_rows = min(512, length)
    steps_count = length // block_rows
    places = jnp.arange(length, dtype=jnp.int32)

    def row_step(carried_grads, block_index):
        key_grad, value_grad = carried_grads
        first_row = block_index * block_rows
        rows_at = first_row + jnp.arange(block_rows, dtype=jnp.int32)
        levels = jnp.zeros((block_rows, length), jnp.int32)
        for bit_index in range(tok_bits):
            levels = levels + (
                rows_at[:, None] // 2**bit_index != places[None, :] // 2**bit_index
            ).astype(jnp.int32)
        weight = jnp.zeros((head_count, block_rows, length), jnp.float32)
        for level_index in range(tok_bits + 1):
            weight = jnp.where(
                (levels == level_index)[None],
                code_weights[:, level_index, :, None] * level_gain(level_index),
                weight,
            )
        weight = jnp.where((places[None, :] <= rows_at[:, None])[None], weight, 0.0)
        scores = jnp.einsum(
            "phd,shd->hps", query_heads, key_heads, preferred_element_type=jnp.float32
        )
        attention = (score_scale * weight * scores).astype(jnp.bfloat16)
        local_out = jnp.einsum(
            "hps,she->phe", attention, value_heads, preferred_element_type=jnp.float32
        )
        dots = jnp.einsum(
            "phe,she->hps", cot_heads, value_heads, preferred_element_type=jnp.float32
        )
        score_grads = (score_scale * weight * dots).astype(jnp.bfloat16)
        local_qgrad = jnp.einsum(
            "hps,shd->phd", score_grads, key_heads, preferred_element_type=jnp.float32
        )
        key_grad = key_grad + jnp.einsum(
            "hps,phd->shd", score_grads, query_heads, preferred_element_type=jnp.float32
        )
        value_grad = value_grad + jnp.einsum(
            "hps,phe->she", attention, cot_heads, preferred_element_type=jnp.float32
        )
        return ((key_grad, value_grad), (local_out, local_qgrad))

    zero_grads = jnp.zeros(head_shape, jnp.float32)
    (key_local, value_local), (local_out, local_qgrad) = lax.scan(
        row_step, (zero_grads, zero_grads), jnp.arange(steps_count, dtype=jnp.int32)
    )
    local_out = local_out.reshape(head_shape)
    local_qgrad = local_qgrad.reshape(head_shape)
    cross_out = jnp.sum(
        row_scale[..., None]
        * jnp.einsum("phd,bhde->bphe", query_heads, bucket, preferred_element_type=jnp.float32),
        axis=0,
    )
    cross_qgrad = jnp.sum(
        row_scale[..., None]
        * jnp.einsum("phe,bhde->bphd", cot_heads, bucket, preferred_element_type=jnp.float32),
        axis=0,
    )
    flat_shape = (length, head_count * head_dim)
    attended = (local_out + cross_out).astype(jnp.bfloat16).reshape(flat_shape)
    grad_query = (local_qgrad + cross_qgrad).astype(jnp.bfloat16).reshape(flat_shape)
    grad_key = (
        (
            key_local
            + jnp.einsum(
                "phe,hde->phd", value_heads, pulled_half, preferred_element_type=jnp.float32
            )
        )
        .astype(jnp.bfloat16)
        .reshape(flat_shape)
    )
    grad_value = (
        (
            value_local
            + jnp.einsum("phd,hde->phe", key_heads, pulled_half, preferred_element_type=jnp.float32)
        )
        .astype(jnp.bfloat16)
        .reshape(flat_shape)
    )
    return (
        lax.all_to_all(attended, "head", split_axis=0, concat_axis=1, tiled=True),
        lax.all_to_all(grad_query, "head", split_axis=0, concat_axis=1, tiled=True),
        lax.all_to_all(grad_key, "head", split_axis=0, concat_axis=1, tiled=True),
        lax.all_to_all(grad_value, "head", split_axis=0, concat_axis=1, tiled=True),
    )


def solution(mesh):
    return jax.shard_map(
        on_device,
        mesh=mesh,
        in_specs=(
            P(("ctx", "head"), None),
            P(("ctx", "head"), None),
            P(("ctx", "head"), None),
            P(("ctx", "head"), None),
            P("head", None, "ctx"),
        ),
        out_specs=(
            P(("ctx", "head"), None),
            P(("ctx", "head"), None),
            P(("ctx", "head"), None),
            P(("ctx", "head"), None),
        ),
        check_vma=False,
    )
```

profile of v0, /device:TPU:1, one launch (start us, length us, event | category | flops | bytes accessed | tf_op | source)
XLA Modules:
  0.0 212.4 jit_solution(3397119964379641207)
XLA Ops:
  0.7 1.9 copy.194
  2.6 6.7 %all-to-all-start.2 = ((bf16[64,8,512]{2,0,1:T(8,128)(2,1)}), bf16[64,8,512]{2,0,1:T(8,128)(2,1)S(1)}, u32[]{:S(2)}, u32[]{:S(2)}) async-start(bf16[64,8,512]{2,0,1:T(8,128)(2,1)} %bitcast.140), calls=%async_computation.2 | async-start | bytes 1048576 | tf_op jit(solution)/shard_map/all_to_all | solution.py:35
  10.4 8.3 %all-to-all-done.2 = bf16[64,8,512]{2,0,1:T(8,128)(2,1)S(1)} async-done(((bf16[64,8,512]{2,0,1:T(8,128)(2,1)}), bf16[64,8,512]{2,0,1:T(8,128)(2,1)S(1)}, u32[]{:S(2)}, u32[]{:S(2)}) %all-to-all-start.2) | async-done | bytes 524320 | tf_op jit(solution)/shard_map/all_to_all | solution.py:35
  18.7 4.4 %all-to-all-start.1 = ((bf16[64,8,512]{2,0,1:T(8,128)(2,1)}), bf16[64,8,512]{2,0,1:T(8,128)(2,1)S(1)}, u32[]{:S(2)}, u32[]{:S(2)}) async-start(bf16[64,8,512]{2,0,1:T(8,128)(2,1)} %bitcast.141), calls=%async_computation.1 | async-start | bytes 1048576 | tf_op jit(solution)/shard_map/all_to_all | solution.py:34
  25.5 6.9 %all-to-all-done.1 = bf16[64,8,512]{2,0,1:T(8,128)(2,1)S(1)} async-done(((bf16[64,8,512]{2,0,1:T(8,128)(2,1)}), bf16[64,8,512]{2,0,1:T(8,128)(2,1)S(1)}, u32[]{:S(2)}, u32[]{:S(2)}) %all-to-all-start.1) | async-done | bytes 524320 | tf_op jit(solution)/shard_map/all_to_all | solution.py:34
  32.5 4.4 %all-to-all-start = ((bf16[64,8,512]{2,0,1:T(8,128)(2,1)}), bf16[64,8,512]{2,0,1:T(8,128)(2,1)S(1)}, u32[]{:S(2)}, u32[]{:S(2)}) async-start(bf16[64,8,512]{2,0,1:T(8,128)(2,1)} %bitcast.142), calls=%async_computation | async-start | bytes 1048576 | tf_op jit(solution)/shard_map/all_to_all | solution.py:33
  36.8 3.9 %broadcast_compare_fusion.9 = (pred[512,512]{1,0:T(8,128)(4,1)}, pred[512,512]{1,0:T(8,128)(4,1)}, pred[512,512]{1,0:T(8,128)(4,1)}, pred[512,512]{1,0:T(8,128)(...) fusion(s32[512]{0:T(512)S(1)} %get-tuple-element.70, ...), kind=kLoop, calls=%fused_computation.46 | loop fusion | flops 9437184 | bytes 2637824 | tf_op jit(solution)/shard_map/while/body/eval_jaxpr/eq | solution.py:104
  40.8 5.4 %all-to-all-done = bf16[64,8,512]{2,0,1:T(8,128)(2,1)S(1)} async-done(((bf16[64,8,512]{2,0,1:T(8,128)(2,1)}), bf16[64,8,512]{2,0,1:T(8,128)(2,1)S(1)}, u32[]{:S(2)}, u32[]{:S(2)}) %all-to-all-start) | async-done | bytes 524320 | tf_op jit(solution)/shard_map/all_to_all | solution.py:33
  46.2 4.4 %all-to-all-start.4 = ((bf16[64,8,512]{2,0,1:T(8,128)(2,1)}), bf16[64,8,512]{2,0,1:T(8,128)(2,1)S(1)}, u32[]{:S(2)}, u32[]{:S(2)}) async-start(bf16[64,8,512]{2,0,1:T(8,128)(2,1)} %bitcast.139), calls=%async_computation.4 | async-start | bytes 1048576 | tf_op jit(solution)/shard_map/all_to_all | solution.py:36
  53.3 6.6 %all-to-all-done.4 = bf16[64,8,512]{2,0,1:T(8,128)(2,1)S(1)} async-done(((bf16[64,8,512]{2,0,1:T(8,128)(2,1)}), bf16[64,8,512]{2,0,1:T(8,128)(2,1)S(1)}, u32[]{:S(2)}, u32[]{:S(2)}) %all-to-all-start.4) | async-done | bytes 524320 | tf_op jit(solution)/shard_map/all_to_all | solution.py:36
  60.1 1.3 copy.112
  61.6 7.4 %multiply_convert_fusion.1 = bf16[4,512,512]{2,1,0:T(8,128)(2,1)} fusion(f32[4,512]{1,0:T(4,128)S(1)} %get-tuple-element.47, f32[4,512]{1,0:T(4,128)S(1)} %get-tuple-element.48, f32[4,512]{1,0:T(4,128)S(1)} %get-tuple-element.49, f32[4,512]{1,0:T(4,128)S(1)} %get-tuple-element.50, f32[4,512]{1,0:T(4,128)S(1)} %get-tuple-element.51, ...), kind=kOutput, calls=%fused_computation.5 | convolution fusion | flops 283115520 | bytes 6111232 | tf_op jit(solution)/shard_map/while/body/eval_jaxpr/phe,she->hps/dot_general | solution.py:116
  69.1 6.4 %multiply_convert_fusion.2 = bf16[4,512,512]{2,1,0:T(8,128)(2,1)S(1)} fusion(f32[4,512]{1,0:T(4,128)S(1)} %get-tuple-element.47, f32[4,512]{1,0:T(4,128)} %copy-done.25, f32[4,512]{1,0:T(4,128)} %copy-done.26, f32[4,512]{1,0:T(4,128)} %copy-done.27, f32[4,512]{1,0:T(4,128)} %copy-done.28, f32[4,512]{1,0:T(4,128)} %copy-done.29, f32[4,512]{1,0:T(4,128)} %copy-done.30, ...), kind=kOutput, calls=%fused_computation.6 | convolution fusion | flops 283115520 | bytes 6111232 | tf_op jit(solution)/shard_map/while/body/eval_jaxpr/phd,shd->hps/dot_general | solution.py:109
  77.0 2.7 %collective-permute-start.1 = (bf16[4,128,128]{2,1,0:T(8,128)(2,1)S(1)}, bf16[4,128,128]{2,1,0:T(8,128)(2,1)S(1)}, u32[]{:S(2)}, u32[]{:S(2)}) collective-permute-start(bf16[4,128,128]{2,1,0:T(8,128)(2,1)S(1)} %fusion.40), channel_id=1, source_target_pairs={{0,16},{16,0},{8,24},{24,8},{32,48},{48,32},{40,56},{56,40},{64,80... | collective-permute-start | bytes 393224 | tf_op jit(solution)/shard_map/ppermute | solution.py:14
  79.7 16.2 %collective-permute-done.1 = bf16[4,128,128]{2,1,0:T(8,128)(2,1)S(1)} collective-permute-done((bf16[4,128,128]{2,1,0:T(8,128)(2,1)S(1)}, bf16[4,128,128]{2,1,0:T(8,128)(2,1)S(1)}, u32[]{:S(2)}, u32[]{:S(2)}) %collective-permute-start.1) | collective-permute-done | bytes 131104 | tf_op jit(solution)/shard_map/ppermute | solution.py:14
  96.0 1.7 collective-permute-start.2
  97.8 2.3 %collective-permute-done.2 = bf16[4,128,128]{2,1,0:T(8,128)(2,1)S(1)} collective-permute-done((bf16[4,128,128]{2,1,0:T(8,128)(2,1)S(1)}, bf16[4,128,128]{2,1,0:T(8,128)(2,1)S(1)}, u32[]{:S(2)}, u32[]{:S(2)}) %collective-permute-start.2) | collective-permute-done | bytes 131104 | tf_op jit(solution)/shard_map/ppermute | solution.py:14
  100.2 3.1 %collective-permute-start.3 = (bf16[4,128,128]{2,1,0:T(8,128)(2,1)S(1)}, bf16[4,128,128]{2,1,0:T(8,128)(2,1)S(1)}, u32[]{:S(2)}, u32[]{:S(2)}) collective-permute-start(bf16[4,128,128]{2,1,0:T(8,128)(2,1)S(1)} %fusion.41), channel_id=1, source_target_pairs={{0,64},{64,0},{8,72},{72,8},{16,80},{80,16},{24,88},{88,24},{32,96... | collective-permute-start | bytes 393224 | tf_op jit(solution)/shard_map/ppermute | solution.py:14
  103.3 3.7 %collective-permute-done.3 = bf16[4,128,128]{2,1,0:T(8,128)(2,1)S(1)} collective-permute-done((bf16[4,128,128]{2,1,0:T(8,128)(2,1)S(1)}, bf16[4,128,128]{2,1,0:T(8,128)(2,1)S(1)}, u32[]{:S(2)}, u32[]{:S(2)}) %collective-permute-start.3) | collective-permute-done | bytes 131104 | tf_op jit(solution)/shard_map/ppermute | solution.py:14
  107.1 6.2 %collective-permute-start.4 = (bf16[4,128,128]{2,1,0:T(8,128)(2,1)S(1)}, bf16[4,128,128]{2,1,0:T(8,128)(2,1)S(1)}, u32[]{:S(2)}, u32[]{:S(2)}) collective-permute-start(bf16[4,128,128]{2,1,0:T(8,128)(2,1)S(1)} %fusion.36), channel_id=1, source_target_pairs={{0,128},{128,0},{8,136},{136,8},{16,144},{144,16},{24,152},{152,24... | collective-permute-start | bytes 393224 | tf_op jit(solution)/shard_map/ppermute | solution.py:14
  116.7 1.9 fusion.1
  118.6 2.5 %copy.98 = f32[512,4,128]{2,0,1:T(8,128)} copy(f32[512,4,128]{0,2,1:T(8,128)} %fusion.1) | data formatting | bytes 2097152 | tf_op jit(solution)/shard_map/reduce_sum | solution.py:137
  121.2 4.5 %collective-permute-done.6 = bf16[4,4,128,128]{2,3,0,1:T(8,128)(2,1)} collective-permute-done((bf16[4,4,128,128]{2,3,0,1:T(8,128)(2,1)}, bf16[4,4,128,128]{2,3,0,1:T(8,128)(2,1)}, u32[]{:S(2)}, u32[]{:S(2)}) %collective-permute-start.6) | collective-permute-done | bytes 524320 | tf_op jit(solution)/shard_map/ppermute | solution.py:14
  125.6 1.5 add_convert_fusion.3
  129.9 2.0 convert_element_type.688
  131.9 9.6 %all-to-all-start.3 = ((bf16[8,64,512]{2,1,0:T(8,128)(2,1)}), bf16[8,64,512]{2,1,0:T(8,128)(2,1)}, u32[]{:S(2)}, u32[]{:S(2)}) async-start(bf16[8,64,512]{2,1,0:T(8,128)(2,1)} %convert_element_type.688), calls=%async_computation.3 | async-start | bytes 1048576 | tf_op jit(solution)/shard_map/all_to_all | solution.py:169
  141.6 3.2 %fusion = f32[512,4,128]{0,2,1:T(8,128)} fusion(f32[5,512,4]{1,0,2:T(8,128)} %copy.93, bf16[5,4,128,128]{3,2,1,0:T(8,128)(2,1)} %copy-done.24, bf16[512,4,128,1]{2,1,0,3:T(4,128)(2,1)} %bitcast.143), kind=kOutput, calls=%fused_computation.1 | convolution fusion | flops 337903616 | bytes 2269184 | tf_op jit(solution)/shard_map/phe,bhde->bphd/dot_general | solution.py:144
  144.8 2.5 %copy.107 = f32[512,4,128]{2,0,1:T(8,128)} copy(f32[512,4,128]{0,2,1:T(8,128)} %fusion) | data formatting | bytes 2097152 | tf_op jit(solution)/shard_map/reduce_sum | solution.py:142
  147.3 1.6 add_convert_fusion.2
  149.6 3.1 %collective-permute-start.8 = (bf16[2,4,128,128]{2,3,0,1:T(8,128)(2,1)}, bf16[2,4,128,128]{2,3,0,1:T(8,128)(2,1)}, u32[]{:S(2)}, u32[]{:S(2)}) collective-permute-start(bf16[2,4,128,128]{2,3,0,1:T(8,128)(2,1)} %pad_maximum_fusion.2), channel_id=1, source_target_pairs={{0,64},{64,0},{8,72},{72,8},{16,80},{80,16},{24,88},{88,24},{32,96... | collective-permute-start | bytes 786440 | tf_op jit(solution)/shard_map/ppermute | solution.py:14
  152.7 2.0 fusion.10
  155.9 2.0 convert_element_type.691
  157.9 7.3 %collective-permute-done.8 = bf16[2,4,128,128]{2,3,0,1:T(8,128)(2,1)} collective-permute-done((bf16[2,4,128,128]{2,3,0,1:T(8,128)(2,1)}, bf16[2,4,128,128]{2,3,0,1:T(8,128)(2,1)}, u32[]{:S(2)}, u32[]{:S(2)}) %collective-permute-start.8) | collective-permute-done | bytes 262176 | tf_op jit(solution)/shard_map/ppermute | solution.py:14
  165.2 1.9 add_convert_fusion.1
  167.1 1.4 collective-permute-start.9
  168.5 5.4 %all-to-all-start.5 = ((bf16[8,64,512]{2,1,0:T(8,128)(2,1)}), bf16[8,64,512]{2,1,0:T(8,128)(2,1)}, u32[]{:S(2)}, u32[]{:S(2)}) async-start(bf16[8,64,512]{2,1,0:T(8,128)(2,1)} %convert_element_type.691), calls=%async_computation.5 | async-start | bytes 1048576 | tf_op jit(solution)/shard_map/all_to_all | solution.py:170
  173.9 2.6 %convolution_bitcast_fusion.1 = f32[512,4,128]{2,0,1:T(8,128)S(1)} fusion(bf16[4,512,512]{2,1,0:T(8,128)(2,1)} %multiply_convert_fusion.1, bf16[512,4,128]{2,1,0:T(4,128)(2,1)} %reshape.3029), kind=kOutput, calls=%fused_computation.13 | convolution fusion | flops 268435456 | bytes 3670016 | tf_op jit(solution)/shard_map/while/body/eval_jaxpr/hps,phd->shd/dot_general | solution.py:123
  176.4 1.4 collective-permute-done.9
  177.8 1.5 fusion.13
  180.5 2.0 all_to_all.118
  183.3 5.0 %all-to-all-start.6 = ((bf16[8,64,512]{2,1,0:T(8,128)(2,1)}), bf16[8,64,512]{2,1,0:T(8,128)(2,1)}, u32[]{:S(2)}, u32[]{:S(2)}) async-start(bf16[8,64,512]{2,1,0:T(8,128)(2,1)} %all_to_all.118), calls=%async_computation.6 | async-start | bytes 1048576 | tf_op jit(solution)/shard_map/all_to_all | solution.py:171
  189.2 1.5 fusion.12
  192.1 5.7 %all-to-all-done.6 = bf16[8,64,512]{2,1,0:T(8,128)(2,1)} async-done(((bf16[8,64,512]{2,1,0:T(8,128)(2,1)}), bf16[8,64,512]{2,1,0:T(8,128)(2,1)}, u32[]{:S(2)}, u32[]{:S(2)}) %all-to-all-start.6) | async-done | bytes 524320 | tf_op jit(solution)/shard_map/all_to_all | solution.py:171
  197.8 4.4 %all-to-all-start.7 = ((bf16[8,64,512]{2,1,0:T(8,128)(2,1)}), bf16[8,64,512]{2,1,0:T(8,128)(2,1)S(1)}, u32[]{:S(2)}, u32[]{:S(2)}) async-start(bf16[8,64,512]{2,1,0:T(8,128)(2,1)} %all_to_all.122), calls=%async_computation.7 | async-start | bytes 1048576 | tf_op jit(solution)/shard_map/all_to_all | solution.py:172
  202.2 1.9 copy.145
  204.1 1.9 copy.146
  205.9 1.9 copy.147
  207.8 3.7 %all-to-all-done.7 = bf16[8,64,512]{2,1,0:T(8,128)(2,1)S(1)} async-done(((bf16[8,64,512]{2,1,0:T(8,128)(2,1)}), bf16[8,64,512]{2,1,0:T(8,128)(2,1)S(1)}, u32[]{:S(2)}, u32[]{:S(2)}) %all-to-all-start.7) | async-done | bytes 524320 | tf_op jit(solution)/shard_map/all_to_all | solution.py:172
  (119 shorter events, 21.3 us)
Async XLA Ops:
  0.6 8.7 %copy-start.22 = (s32[4,15,512]{2,0,1:T(4,128)S(1)}, s32[4,15,512]{2,0,1:T(4,128)}, u32[]{:S(2)}) copy-start(s32[4,15,512]{2,0,1:T(4,128)} %param.9) | copy-start | bytes 368644
  0.6 8.9 %copy-start.8 = (bf16[64,4096]{1,0:T(8,128)(2,1)S(1)}, bf16[64,4096]{1,0:T(8,128)(2,1)}, u32[]{:S(2)}) copy-start(bf16[64,4096]{1,0:T(8,128)(2,1)} %param.6) | copy-start | bytes 1572868
  2.6 21.1 %copy-start.9 = (bf16[64,4096]{1,0:T(8,128)(2,1)S(1)}, bf16[64,4096]{1,0:T(8,128)(2,1)}, u32[]{:S(2)}) copy-start(bf16[64,4096]{1,0:T(8,128)(2,1)} %param.5) | copy-start | bytes 1572868
  2.6 16.1 %all-to-all-start.2 = ((bf16[64,8,512]{2,0,1:T(8,128)(2,1)}), bf16[64,8,512]{2,0,1:T(8,128)(2,1)S(1)}, u32[]{:S(2)}, u32[]{:S(2)}) async-start(bf16[64,8,512]{2,0,1:T(8,128)(2,1)} %bitcast.140), calls=%async_computation.2 | async-start | bytes 1048576 | tf_op jit(solution)/shard_map/all_to_all | solution.py:35
  9.3 15.2 %copy-start.10 = (bf16[64,4096]{1,0:T(8,128)(2,1)S(1)}, bf16[64,4096]{1,0:T(8,128)(2,1)}, u32[]{:S(2)}) copy-start(bf16[64,4096]{1,0:T(8,128)(2,1)} %param.8) | copy-start | bytes 1572868
  18.7 13.7 %all-to-all-start.1 = ((bf16[64,8,512]{2,0,1:T(8,128)(2,1)}), bf16[64,8,512]{2,0,1:T(8,128)(2,1)S(1)}, u32[]{:S(2)}, u32[]{:S(2)}) async-start(bf16[64,8,512]{2,0,1:T(8,128)(2,1)} %bitcast.141), calls=%async_computation.1 | async-start | bytes 1048576 | tf_op jit(solution)/shard_map/all_to_all | solution.py:34
  25.5 35.9 %copy-start.11 = (pred[512,512]{1,0:T(8,128)(4,1)}, pred[512,512]{1,0:T(8,128)(4,1)S(1)}, u32[]{:S(2)}) copy-start(pred[512,512]{1,0:T(8,128)(4,1)S(1)} %iota_compare_fusion.1) | copy-start | bytes 786436
  32.5 13.7 %all-to-all-start = ((bf16[64,8,512]{2,0,1:T(8,128)(2,1)}), bf16[64,8,512]{2,0,1:T(8,128)(2,1)S(1)}, u32[]{:S(2)}, u32[]{:S(2)}) async-start(bf16[64,8,512]{2,0,1:T(8,128)(2,1)} %bitcast.142), calls=%async_computation | async-start | bytes 1048576 | tf_op jit(solution)/shard_map/all_to_all | solution.py:33
  46.2 13.7 %all-to-all-start.4 = ((bf16[64,8,512]{2,0,1:T(8,128)(2,1)}), bf16[64,8,512]{2,0,1:T(8,128)(2,1)S(1)}, u32[]{:S(2)}, u32[]{:S(2)}) async-start(bf16[64,8,512]{2,0,1:T(8,128)(2,1)} %bitcast.139), calls=%async_computation.4 | async-start | bytes 1048576 | tf_op jit(solution)/shard_map/all_to_all | solution.py:36
  50.6 10.8 %copy-start.25 = (f32[4,512]{1,0:T(4,128)}, f32[4,512]{1,0:T(4,128)S(1)}, u32[]{:S(2)}) copy-start(f32[4,512]{1,0:T(4,128)S(1)} %get-tuple-element.48) | copy-start | bytes 24580
  50.6 10.8 %copy-start.26 = (f32[4,512]{1,0:T(4,128)}, f32[4,512]{1,0:T(4,128)S(1)}, u32[]{:S(2)}) copy-start(f32[4,512]{1,0:T(4,128)S(1)} %get-tuple-element.49) | copy-start | bytes 24580
  50.6 10.8 %copy-start.27 = (f32[4,512]{1,0:T(4,128)}, f32[4,512]{1,0:T(4,128)S(1)}, u32[]{:S(2)}) copy-start(f32[4,512]{1,0:T(4,128)S(1)} %get-tuple-element.50) | copy-start | bytes 24580
  50.6 10.8 %copy-start.28 = (f32[4,512]{1,0:T(4,128)}, f32[4,512]{1,0:T(4,128)S(1)}, u32[]{:S(2)}) copy-start(f32[4,512]{1,0:T(4,128)S(1)} %get-tuple-element.51) | copy-start | bytes 24580
  50.6 10.8 %copy-start.29 = (f32[4,512]{1,0:T(4,128)}, f32[4,512]{1,0:T(4,128)S(1)}, u32[]{:S(2)}) copy-start(f32[4,512]{1,0:T(4,128)S(1)} %get-tuple-element.52) | copy-start | bytes 24580
  50.6 10.8 %copy-start.30 = (f32[4,512]{1,0:T(4,128)}, f32[4,512]{1,0:T(4,128)S(1)}, u32[]{:S(2)}) copy-start(f32[4,512]{1,0:T(4,128)S(1)} %get-tuple-element.53) | copy-start | bytes 24580
  50.6 10.8 %copy-start.31 = (f32[4,512]{1,0:T(4,128)}, f32[4,512]{1,0:T(4,128)S(1)}, u32[]{:S(2)}) copy-start(f32[4,512]{1,0:T(4,128)S(1)} %get-tuple-element.54) | copy-start | bytes 24580
  50.6 10.8 %copy-start.32 = (f32[4,512]{1,0:T(4,128)}, f32[4,512]{1,0:T(4,128)S(1)}, u32[]{:S(2)}) copy-start(f32[4,512]{1,0:T(4,128)S(1)} %get-tuple-element.55) | copy-start | bytes 24580
  51.9 25.0 %collective-permute-start = (bf16[4,128,128]{2,1,0:T(8,128)(2,1)}, bf16[4,128,128]{2,1,0:T(8,128)(2,1)S(1)}, u32[]{:S(2)}, u32[]{:S(2)}) collective-permute-start(bf16[4,128,128]{2,1,0:T(8,128)(2,1)} %get-tuple-element.66), channel_id=1, source_target_pairs={{0,8},{8,0},{16,24},{24,16},{32,40},{40,32},{48,56},{56,48},{64,72... | collective-permute-start | bytes 393224 | tf_op jit(solution)/shard_map/ppermute | solution.py:14
  61.5 7.5 %copy-start.6 = (bf16[512,4,128]{2,1,0:T(4,128)(2,1)S(1)}, bf16[512,4,128]{2,1,0:T(4,128)(2,1)}, u32[]{:S(2)}) copy-start(bf16[512,4,128]{2,1,0:T(4,128)(2,1)} %reshape.3029) | copy-start | bytes 1572868
  61.5 7.5 %copy-start.12 = (pred[512,512]{1,0:T(8,128)(4,1)S(1)}, pred[512,512]{1,0:T(8,128)(4,1)}, u32[]{:S(2)}) copy-start(pred[512,512]{1,0:T(8,128)(4,1)} %get-tuple-element.56) | copy-start | bytes 786436
  61.5 7.5 %copy-start.13 = (pred[512,512]{1,0:T(8,128)(4,1)S(1)}, pred[512,512]{1,0:T(8,128)(4,1)}, u32[]{:S(2)}) copy-start(pred[512,512]{1,0:T(8,128)(4,1)} %get-tuple-element.57) | copy-start | bytes 786436
  61.5 7.5 %copy-start.14 = (pred[512,512]{1,0:T(8,128)(4,1)S(1)}, pred[512,512]{1,0:T(8,128)(4,1)}, u32[]{:S(2)}) copy-start(pred[512,512]{1,0:T(8,128)(4,1)} %get-tuple-element.58) | copy-start | bytes 786436
  61.5 7.5 %copy-start.15 = (pred[512,512]{1,0:T(8,128)(4,1)S(1)}, pred[512,512]{1,0:T(8,128)(4,1)}, u32[]{:S(2)}) copy-start(pred[512,512]{1,0:T(8,128)(4,1)} %get-tuple-element.59) | copy-start | bytes 786436
  61.5 7.5 %copy-start.16 = (pred[512,512]{1,0:T(8,128)(4,1)S(1)}, pred[512,512]{1,0:T(8,128)(4,1)}, u32[]{:S(2)}) copy-start(pred[512,512]{1,0:T(8,128)(4,1)} %get-tuple-element.60) | copy-start | bytes 786436
  61.5 7.5 %copy-start.17 = (pred[512,512]{1,0:T(8,128)(4,1)S(1)}, pred[512,512]{1,0:T(8,128)(4,1)}, u32[]{:S(2)}) copy-start(pred[512,512]{1,0:T(8,128)(4,1)} %get-tuple-element.61) | copy-start | bytes 786436
  61.5 7.5 %copy-start.18 = (pred[512,512]{1,0:T(8,128)(4,1)S(1)}, pred[512,512]{1,0:T(8,128)(4,1)}, u32[]{:S(2)}) copy-start(pred[512,512]{1,0:T(8,128)(4,1)} %get-tuple-element.62) | copy-start | bytes 786436
  61.5 7.5 %copy-start.19 = (pred[512,512]{1,0:T(8,128)(4,1)S(1)}, pred[512,512]{1,0:T(8,128)(4,1)}, u32[]{:S(2)}) copy-start(pred[512,512]{1,0:T(8,128)(4,1)} %get-tuple-element.63) | copy-start | bytes 786436
  61.6 7.5 %copy-start.20 = (pred[512,512]{1,0:T(8,128)(4,1)S(1)}, pred[512,512]{1,0:T(8,128)(4,1)}, u32[]{:S(2)}) copy-start(pred[512,512]{1,0:T(8,128)(4,1)} %get-tuple-element.64) | copy-start | bytes 786436
  61.6 7.5 %copy-start.21 = (pred[512,512]{1,0:T(8,128)(4,1)S(1)}, pred[512,512]{1,0:T(8,128)(4,1)}, u32[]{:S(2)}) copy-start(pred[512,512]{1,0:T(8,128)(4,1)} %get-tuple-element.65) | copy-start | bytes 786436
  69.1 6.4 %copy-start.7 = (f32[512,4,128]{0,2,1:T(8,128)S(1)}, f32[512,4,128]{0,2,1:T(8,128)}, u32[]{:S(2)}) copy-start(f32[512,4,128]{0,2,1:T(8,128)} %copy.112) | copy-start | bytes 3145732
  69.1 6.4 %copy-start.23 = (f32[5,512,4]{1,0,2:T(8,128)S(1)}, f32[5,512,4]{1,0,2:T(8,128)}, u32[]{:S(2)}) copy-start(f32[5,512,4]{1,0,2:T(8,128)} %copy.93) | copy-start | bytes 122884
  76.4 37.1 %copy-start.1 = (f32[5,4,128,128]{2,3,0,1:T(8,128)}, f32[5,4,128,128]{2,3,0,1:T(8,128)S(1)}, u32[]{:S(2)}) copy-start(f32[5,4,128,128]{2,3,0,1:T(8,128)S(1)} %get-tuple-element.69) | copy-start | bytes 3932164
  76.4 36.9 %collective-permute-start.5 = (bf16[5,4,128,128]{2,3,0,1:T(8,128)(2,1)S(1)}, bf16[5,4,128,128]{2,3,0,1:T(8,128)(2,1)S(1)}, u32[]{:S(2)}, u32[]{:S(2)}) collective-permute-start(bf16[5,4,128,128]{2,3,0,1:T(8,128)(2,1)S(1)} %get-tuple-element.68), channel_id=1, source_target_pairs={{0,8},{8,0},{16,24},{24,16},{32,40},{40,32},{48,56},{56,48},{64,72... | collective-permute-start | bytes 1966088 | tf_op jit(solution)/shard_map/ppermute | solution.py:14
  77.0 19.0 %collective-permute-start.1 = (bf16[4,128,128]{2,1,0:T(8,128)(2,1)S(1)}, bf16[4,128,128]{2,1,0:T(8,128)(2,1)S(1)}, u32[]{:S(2)}, u32[]{:S(2)}) collective-permute-start(bf16[4,128,128]{2,1,0:T(8,128)(2,1)S(1)} %fusion.40), channel_id=1, source_target_pairs={{0,16},{16,0},{8,24},{24,8},{32,48},{48,32},{40,56},{56,40},{64,80... | collective-permute-start | bytes 393224 | tf_op jit(solution)/shard_map/ppermute | solution.py:14
  96.0 4.1 %collective-permute-start.2 = (bf16[4,128,128]{2,1,0:T(8,128)(2,1)S(1)}, bf16[4,128,128]{2,1,0:T(8,128)(2,1)S(1)}, u32[]{:S(2)}, u32[]{:S(2)}) collective-permute-start(bf16[4,128,128]{2,1,0:T(8,128)(2,1)S(1)} %fusion.87), channel_id=1, source_target_pairs={{0,32},{32,0},{8,40},{40,8},{16,48},{48,16},{24,56},{56,24},{64,96... | collective-permute-start | bytes 393224 | tf_op jit(solution)/shard_map/ppermute | solution.py:14
  100.2 6.8 %collective-permute-start.3 = (bf16[4,128,128]{2,1,0:T(8,128)(2,1)S(1)}, bf16[4,128,128]{2,1,0:T(8,128)(2,1)S(1)}, u32[]{:S(2)}, u32[]{:S(2)}) collective-permute-start(bf16[4,128,128]{2,1,0:T(8,128)(2,1)S(1)} %fusion.41), channel_id=1, source_target_pairs={{0,64},{64,0},{8,72},{72,8},{16,80},{80,16},{24,88},{88,24},{32,96... | collective-permute-start | bytes 393224 | tf_op jit(solution)/shard_map/ppermute | solution.py:14
  107.1 8.7 %collective-permute-start.4 = (bf16[4,128,128]{2,1,0:T(8,128)(2,1)S(1)}, bf16[4,128,128]{2,1,0:T(8,128)(2,1)S(1)}, u32[]{:S(2)}, u32[]{:S(2)}) collective-permute-start(bf16[4,128,128]{2,1,0:T(8,128)(2,1)S(1)} %fusion.36), channel_id=1, source_target_pairs={{0,128},{128,0},{8,136},{136,8},{16,144},{144,16},{24,152},{152,24... | collective-permute-start | bytes 393224 | tf_op jit(solution)/shard_map/ppermute | solution.py:14
  115.0 10.6 %collective-permute-start.6 = (bf16[4,4,128,128]{2,3,0,1:T(8,128)(2,1)}, bf16[4,4,128,128]{2,3,0,1:T(8,128)(2,1)}, u32[]{:S(2)}, u32[]{:S(2)}) collective-permute-start(bf16[4,4,128,128]{2,3,0,1:T(8,128)(2,1)} %pad_maximum_fusion), channel_id=1, source_target_pairs={{0,16},{16,0},{8,24},{24,8},{32,48},{48,32},{40,56},{56,40},{64,80... | collective-permute-start | bytes 1572872 | tf_op jit(solution)/shard_map/ppermute | solution.py:14
  121.1 6.8 %copy-start.4 = (f32[512,4,128]{2,0,1:T(8,128)S(1)}, f32[512,4,128]{2,0,1:T(8,128)}, u32[]{:S(2)}) copy-start(f32[512,4,128]{2,0,1:T(8,128)} %copy.98) | copy-start | bytes 3145732
  128.0 19.4 %collective-permute-start.7 = (bf16[3,4,128,128]{2,3,0,1:T(8,128)(2,1)}, bf16[3,4,128,128]{2,3,0,1:T(8,128)(2,1)S(1)}, u32[]{:S(2)}, u32[]{:S(2)}) collective-permute-start(bf16[3,4,128,128]{2,3,0,1:T(8,128)(2,1)} %pad_maximum_fusion.1), channel_id=1, source_target_pairs={{0,32},{32,0},{8,40},{40,8},{16,48},{48,16},{24,56},{56,24},{64,96... | collective-permute-start | bytes 1179656 | tf_op jit(solution)/shard_map/ppermute | solution.py:14
  131.9 36.5 %all-to-all-start.3 = ((bf16[8,64,512]{2,1,0:T(8,128)(2,1)}), bf16[8,64,512]{2,1,0:T(8,128)(2,1)}, u32[]{:S(2)}, u32[]{:S(2)}) async-start(bf16[8,64,512]{2,1,0:T(8,128)(2,1)} %convert_element_type.688), calls=%async_computation.3 | async-start | bytes 1048576 | tf_op jit(solution)/shard_map/all_to_all | solution.py:169
  147.3 5.4 %copy-start = (bf16[4,512,512]{2,1,0:T(8,128)(2,1)S(1)}, bf16[4,512,512]{2,1,0:T(8,128)(2,1)}, u32[]{:S(2)}) copy-start(bf16[4,512,512]{2,1,0:T(8,128)(2,1)} %multiply_convert_fusion.1) | copy-start | bytes 6291460
  149.6 15.6 %collective-permute-start.8 = (bf16[2,4,128,128]{2,3,0,1:T(8,128)(2,1)}, bf16[2,4,128,128]{2,3,0,1:T(8,128)(2,1)}, u32[]{:S(2)}, u32[]{:S(2)}) collective-permute-start(bf16[2,4,128,128]{2,3,0,1:T(8,128)(2,1)} %pad_maximum_fusion.2), channel_id=1, source_target_pairs={{0,64},{64,0},{8,72},{72,8},{16,80},{80,16},{24,88},{88,24},{32,96... | collective-permute-start | bytes 786440 | tf_op jit(solution)/shard_map/ppermute | solution.py:14
  167.1 10.7 %collective-permute-start.9 = (bf16[1,4,128,128]{2,3,0,1:T(8,128)(2,1)}, bf16[1,4,128,128]{2,3,0,1:T(8,128)(2,1)}, u32[]{:S(2)}, u32[]{:S(2)}) collective-permute-start(bf16[1,4,128,128]{2,3,0,1:T(8,128)(2,1)} %add_convert_fusion.1), channel_id=1, source_target_pairs={{0,128},{128,0},{8,136},{136,8},{16,144},{144,16},{24,152},{152,24... | collective-permute-start | bytes 393224 | tf_op jit(solution)/shard_map/ppermute | solution.py:14
  168.5 14.9 %all-to-all-start.5 = ((bf16[8,64,512]{2,1,0:T(8,128)(2,1)}), bf16[8,64,512]{2,1,0:T(8,128)(2,1)}, u32[]{:S(2)}, u32[]{:S(2)}) async-start(bf16[8,64,512]{2,1,0:T(8,128)(2,1)} %convert_element_type.691), calls=%async_computation.5 | async-start | bytes 1048576 | tf_op jit(solution)/shard_map/all_to_all | solution.py:170
  179.3 9.1 %copy-start.3 = (bf16[512,4,128]{2,1,0:T(4,128)(2,1)S(1)}, bf16[512,4,128]{2,1,0:T(4,128)(2,1)}, u32[]{:S(2)}) copy-start(bf16[512,4,128]{2,1,0:T(4,128)(2,1)} %copy-done.2) | copy-start | bytes 1572868
  183.3 14.5 %all-to-all-start.6 = ((bf16[8,64,512]{2,1,0:T(8,128)(2,1)}), bf16[8,64,512]{2,1,0:T(8,128)(2,1)}, u32[]{:S(2)}, u32[]{:S(2)}) async-start(bf16[8,64,512]{2,1,0:T(8,128)(2,1)} %all_to_all.118), calls=%async_computation.6 | async-start | bytes 1048576 | tf_op jit(solution)/shard_map/all_to_all | solution.py:171
  197.8 13.7 %all-to-all-start.7 = ((bf16[8,64,512]{2,1,0:T(8,128)(2,1)}), bf16[8,64,512]{2,1,0:T(8,128)(2,1)S(1)}, u32[]{:S(2)}, u32[]{:S(2)}) async-start(bf16[8,64,512]{2,1,0:T(8,128)(2,1)} %all_to_all.122), calls=%async_computation.7 | async-start | bytes 1048576 | tf_op jit(solution)/shard_map/all_to_all | solution.py:172
  (3 other events, 3.1 us)
where the time goes:
time: 214 us; the launch traced here: 212 us
  waiting for transfers between devices  73.3 us (34%)
  starting transfers between devices  63.8 us (30%)
  local copies, waits for them, and re-layouts  32.1 us (15%)
  matrix products  29.9 us (14%)
  other arithmetic  12.1 us (6%)
    ppermute x10, waiting for transfers between devices, swapped(): return lax.ppermute(block, axis, route)  35.7 us
    ppermute x10, starting transfers between devices, swapped(): return lax.ppermute(block, axis, route)  19.5 us
    all_to_all x1, starting transfers between devices, on_device(): lax.all_to_all(attended, 'head', split_axis=0, concat_axis=1, tiled=True)  9.64 us
    all_to_all x1, waiting for transfers between devices, on_device(): lax.all_to_all(value_input, 'head', split_axis=1, concat_axis=0, tiled=True)  8.33 us
    dot_general x1, matrix products, row_step(): jnp.einsum('phe,she->hps', cot_heads, value_heads, preferred_element_type...  7.41 us
    all_to_all x1, waiting for transfers between devices, on_device(): lax.all_to_all(key_input, 'head', split_axis=1, concat_axis=0, tiled=True)  6.93 us
    all_to_all x1, starting transfers between devices, on_device(): lax.all_to_all(value_input, 'head', split_axis=1, concat_axis=0, tiled=True)  6.73 us
    all_to_all x1, waiting for transfers between devices, on_device(): lax.all_to_all(cotangent, 'head', split_axis=1, concat_axis=0, tiled=True)  6.63 us
  transfers between devices with their start and end apart: 18, of which 14 were waited for; matrix products, arithmetic and copies ran while one was open for 30% of the time, Pallas kernels for 0%

commit v1 on v0

--- a/solution.py
+++ b/solution.py
@@ -33,7 +33,12 @@
         lax.all_to_all(query_input, "head", split_axis=1, concat_axis=0, tiled=True),
         lax.all_to_all(key_input, "head", split_axis=1, concat_axis=0, tiled=True),
         lax.all_to_all(value_input, "head", split_axis=1, concat_axis=0, tiled=True),
-        lax.all_to_all(cotangent, "head", split_axis=1, concat_axis=0, tiled=True),
+        jnp.concatenate(
+            lax.all_to_all(
+                jnp.stack(jnp.split(cotangent, lax.axis_size("head"), axis=1)), "head", 0, 0
+            ),
+            axis=0,
+        ),
     )
     head_count = level_codes.shape[0]
     total_levels = level_codes.shape[1]

time: 214 us -> 213 us (level)
  waiting for transfers between devices: 73.3 us -> 66.8 us
  local copies, waits for them, and re-layouts: 32.1 us -> 37.3 us
    all_to_all x1, waiting for transfers between devices: 8.33 us -> 3.74 us  [on_device(): lax.all_to_all(value_input, 'head', split_axis=1, concat_axis=0, tiled=True)]
    unnamed x66 -> x75, local copies, waits for them, and re-layouts: 1.66 us -> 6.08 us
  transfers between devices with their start and end apart: 18 -> 18, of which waited for: 14 -> 14; matrix products, arithmetic and copies ran while one was open for 30% -> 33% of each run, Pallas kernels for 0% -> 0%
where the time goes in v1:
time: 213 us; the launch traced here: 211 us
  waiting for transfers between devices  66.8 us (31%)
  starting transfers between devices  63.6 us (30%)
  local copies, waits for them, and re-layouts  37.3 us (18%)
  matrix products  29 us (14%)
  other arithmetic  13.4 us (6%)
    ppermute x10, waiting for transfers between devices, swapped(): return lax.ppermute(block, axis, route)  35.7 us
    ppermute x10, starting transfers between devices, swapped(): return lax.ppermute(block, axis, route)  19.5 us
    all_to_all x1, starting transfers between devices, on_device(): lax.all_to_all(attended, 'head', split_axis=0, concat_axis=1, tiled=True)  9.62 us
    dot_general x1, matrix products, row_step(): jnp.einsum('phd,shd->hps', query_heads, key_heads, preferred_element_type...  6.81 us
    all_to_all x1, waiting for transfers between devices, on_device(): lax.all_to_all(key_input, 'head', split_axis=1, concat_axis=0, tiled=True)  6.62 us
    all_to_all x1, starting transfers between devices, on_device(): lax.all_to_all(value_input, 'head', split_axis=1, concat_axis=0, tiled=True)  6.6 us
    dot_general x1, matrix products, row_step(): jnp.einsum('phe,she->hps', cot_heads, value_heads, preferred_element_type...  6.55 us
    all_to_all x1, waiting for transfers between devices, on_device(): lax.all_to_all(grad_key, 'head', split_axis=0, concat_axis=1, tiled=True)  6.28 us
  transfers between devices with their start and end apart: 18, of which 14 were waited for; matrix products, arithmetic and copies ran while one was open for 33% of the time, Pallas kernels for 0%

profile of v1, /device:TPU:1, one launch (start us, length us, event | category | flops | bytes accessed | tf_op | source)
XLA Modules:
  0.0 211.3 jit_solution(2539490356993156743)
XLA Ops:
  0.7 2.0 copy.176
  2.6 6.6 %all-to-all-start.2 = ((bf16[64,8,512]{2,0,1:T(8,128)(2,1)}), bf16[64,8,512]{2,0,1:T(8,128)(2,1)S(1)}, u32[]{:S(2)}, u32[]{:S(2)}) async-start(bf16[64,8,512]{2,0,1:T(8,128)(2,1)} %bitcast.147), calls=%async_computation.2 | async-start | bytes 1048576 | tf_op jit(solution)/shard_map/all_to_all | solution.py:35
  14.9 3.7 %all-to-all-done.2 = bf16[64,8,512]{2,0,1:T(8,128)(2,1)S(1)} async-done(((bf16[64,8,512]{2,0,1:T(8,128)(2,1)}), bf16[64,8,512]{2,0,1:T(8,128)(2,1)S(1)}, u32[]{:S(2)}, u32[]{:S(2)}) %all-to-all-start.2) | async-done | bytes 524320 | tf_op jit(solution)/shard_map/all_to_all | solution.py:35
  18.6 4.4 %all-to-all-start.1 = ((bf16[64,8,512]{2,0,1:T(8,128)(2,1)}), bf16[64,8,512]{2,0,1:T(8,128)(2,1)S(1)}, u32[]{:S(2)}, u32[]{:S(2)}) async-start(bf16[64,8,512]{2,0,1:T(8,128)(2,1)} %bitcast.148), calls=%async_computation.1 | async-start | bytes 1048576 | tf_op jit(solution)/shard_map/all_to_all | solution.py:34
  25.7 6.6 %all-to-all-done.1 = bf16[64,8,512]{2,0,1:T(8,128)(2,1)S(1)} async-done(((bf16[64,8,512]{2,0,1:T(8,128)(2,1)}), bf16[64,8,512]{2,0,1:T(8,128)(2,1)S(1)}, u32[]{:S(2)}, u32[]{:S(2)}) %all-to-all-start.1) | async-done | bytes 524320 | tf_op jit(solution)/shard_map/all_to_all | solution.py:34
  32.4 4.4 %all-to-all-start.4 = ((bf16[8,64,512]{2,1,0:T(8,128)(2,1)}), bf16[8,64,512]{2,1,0:T(8,128)(2,1)S(1)}, u32[]{:S(2)}, u32[]{:S(2)}) async-start(bf16[8,64,512]{2,1,0:T(8,128)(2,1)} %bitcast_dynamic-update-slice_fusion), calls=%async_computation.4 | async-start | bytes 1048576 | tf_op jit(solution)/shard_map/all_to_all | solution.py:37
  36.7 3.9 %broadcast_compare_fusion.9 = (pred[512,512]{1,0:T(8,128)(4,1)}, pred[512,512]{1,0:T(8,128)(4,1)}, pred[512,512]{1,0:T(8,128)(4,1)}, pred[512,512]{1,0:T(8,128)(...) fusion(s32[512]{0:T(512)S(1)} %get-tuple-element.70, ...), kind=kLoop, calls=%fused_computation.44 | loop fusion | flops 9437184 | bytes 2637824 | tf_op jit(solution)/shard_map/while/body/eval_jaxpr/eq | solution.py:109
  40.6 5.5 %all-to-all-done.4 = bf16[8,64,512]{2,1,0:T(8,128)(2,1)S(1)} async-done(((bf16[8,64,512]{2,1,0:T(8,128)(2,1)}), bf16[8,64,512]{2,1,0:T(8,128)(2,1)S(1)}, u32[]{:S(2)}, u32[]{:S(2)}) %all-to-all-start.4) | async-done | bytes 524320 | tf_op jit(solution)/shard_map/all_to_all | solution.py:37
  46.1 4.4 %all-to-all-start = ((bf16[64,8,512]{2,0,1:T(8,128)(2,1)}), bf16[64,8,512]{2,0,1:T(8,128)(2,1)S(1)}, u32[]{:S(2)}, u32[]{:S(2)}) async-start(bf16[64,8,512]{2,0,1:T(8,128)(2,1)} %bitcast.149), calls=%async_computation | async-start | bytes 1048576 | tf_op jit(solution)/shard_map/all_to_all | solution.py:33
  52.4 1.3 copy.105
  55.4 4.4 %all-to-all-done = bf16[64,8,512]{2,0,1:T(8,128)(2,1)S(1)} async-done(((bf16[64,8,512]{2,0,1:T(8,128)(2,1)}), bf16[64,8,512]{2,0,1:T(8,128)(2,1)S(1)}, u32[]{:S(2)}, u32[]{:S(2)}) %all-to-all-start) | async-done | bytes 524320 | tf_op jit(solution)/shard_map/all_to_all | solution.py:33
  60.9 6.8 %multiply_convert_fusion.2 = bf16[4,512,512]{2,1,0:T(8,128)(2,1)S(1)} fusion(f32[4,512]{1,0:T(4,128)S(1)} %get-tuple-element.47, f32[4,512]{1,0:T(4,128)} %get-tuple-element.48, f32[4,512]{1,0:T(4,128)} %get-tuple-element.49, f32[4,512]{1,0:T(4,128)} %get-tuple-element.50, f32[4,512]{1,0:T(4,128)} %get-tuple-element.51, f32[4,512]{1,0:T(4,128)} %get-tuple-element.52, ...), kind=kOutput, calls=%fused_computation.6 | convolution fusion | flops 283115520 | bytes 6111232 | tf_op jit(solution)/shard_map/while/body/eval_jaxpr/phd,shd->hps/dot_general | solution.py:114
  68.0 6.6 %multiply_convert_fusion.1 = bf16[4,512,512]{2,1,0:T(8,128)(2,1)} fusion(bf16[512,4,128]{0,2,1:T(8,128)(2,1)S(1)} %copy-done.5, f32[4,512]{1,0:T(4,128)S(1)} %get-tuple-element.47, f32[4,512]{1,0:T(4,128)S(1)} %copy-done.26, f32[4,512]{1,0:T(4,128)S(1)} %copy-done.27, f32[4,512]{1,0:T(4,128)S(1)} %copy-done.28, f32[4,512]{1,0:T(4,128)S(1)} %copy-done.29, ...), kind=kOutput, calls=%fused_computation.5 | convolution fusion | flops 283115520 | bytes 6111232 | tf_op jit(solution)/shard_map/while/body/eval_jaxpr/phe,she->hps/dot_general | solution.py:121
  76.0 2.7 %collective-permute-start.1 = (bf16[4,128,128]{2,1,0:T(8,128)(2,1)S(1)}, bf16[4,128,128]{2,1,0:T(8,128)(2,1)S(1)}, u32[]{:S(2)}, u32[]{:S(2)}) collective-permute-start(bf16[4,128,128]{2,1,0:T(8,128)(2,1)S(1)} %fusion.38), channel_id=1, source_target_pairs={{0,16},{16,0},{8,24},{24,8},{32,48},{48,32},{40,56},{56,40},{64,80... | collective-permute-start | bytes 393224 | tf_op jit(solution)/shard_map/ppermute | solution.py:14
  78.7 16.2 %collective-permute-done.1 = bf16[4,128,128]{2,1,0:T(8,128)(2,1)S(1)} collective-permute-done((bf16[4,128,128]{2,1,0:T(8,128)(2,1)S(1)}, bf16[4,128,128]{2,1,0:T(8,128)(2,1)S(1)}, u32[]{:S(2)}, u32[]{:S(2)}) %collective-permute-start.1) | collective-permute-done | bytes 131104 | tf_op jit(solution)/shard_map/ppermute | solution.py:14
  95.0 1.7 collective-permute-start.2
  96.8 2.3 %collective-permute-done.2 = bf16[4,128,128]{2,1,0:T(8,128)(2,1)S(1)} collective-permute-done((bf16[4,128,128]{2,1,0:T(8,128)(2,1)S(1)}, bf16[4,128,128]{2,1,0:T(8,128)(2,1)S(1)}, u32[]{:S(2)}, u32[]{:S(2)}) %collective-permute-start.2) | collective-permute-done | bytes 131104 | tf_op jit(solution)/shard_map/ppermute | solution.py:14
  99.2 3.1 %collective-permute-start.3 = (bf16[4,128,128]{2,1,0:T(8,128)(2,1)S(1)}, bf16[4,128,128]{2,1,0:T(8,128)(2,1)S(1)}, u32[]{:S(2)}, u32[]{:S(2)}) collective-permute-start(bf16[4,128,128]{2,1,0:T(8,128)(2,1)S(1)} %fusion.39), channel_id=1, source_target_pairs={{0,64},{64,0},{8,72},{72,8},{16,80},{80,16},{24,88},{88,24},{32,96... | collective-permute-start | bytes 393224 | tf_op jit(solution)/shard_map/ppermute | solution.py:14
  102.3 3.7 %collective-permute-done.3 = bf16[4,128,128]{2,1,0:T(8,128)(2,1)S(1)} collective-permute-done((bf16[4,128,128]{2,1,0:T(8,128)(2,1)S(1)}, bf16[4,128,128]{2,1,0:T(8,128)(2,1)S(1)}, u32[]{:S(2)}, u32[]{:S(2)}) %collective-permute-start.3) | collective-permute-done | bytes 131104 | tf_op jit(solution)/shard_map/ppermute | solution.py:14
  106.1 6.2 %collective-permute-start.4 = (bf16[4,128,128]{2,1,0:T(8,128)(2,1)S(1)}, bf16[4,128,128]{2,1,0:T(8,128)(2,1)S(1)}, u32[]{:S(2)}, u32[]{:S(2)}) collective-permute-start(bf16[4,128,128]{2,1,0:T(8,128)(2,1)S(1)} %fusion.34), channel_id=1, source_target_pairs={{0,128},{128,0},{8,136},{136,8},{16,144},{144,16},{24,152},{152,24... | collective-permute-start | bytes 393224 | tf_op jit(solution)/shard_map/ppermute | solution.py:14
  115.7 1.9 fusion.1
  117.6 2.5 %copy.92 = f32[512,4,128]{2,0,1:T(8,128)} copy(f32[512,4,128]{0,2,1:T(8,128)} %fusion.1) | data formatting | bytes 2097152 | tf_op jit(solution)/shard_map/reduce_sum | solution.py:142
  120.1 4.5 %collective-permute-done.6 = bf16[4,4,128,128]{2,3,0,1:T(8,128)(2,1)} collective-permute-done((bf16[4,4,128,128]{2,3,0,1:T(8,128)(2,1)}, bf16[4,4,128,128]{2,3,0,1:T(8,128)(2,1)}, u32[]{:S(2)}, u32[]{:S(2)}) %collective-permute-start.6) | collective-permute-done | bytes 524320 | tf_op jit(solution)/shard_map/ppermute | solution.py:14
  124.6 1.5 add_convert_fusion.3
  128.8 2.0 convert_element_type.691
  130.9 9.6 %all-to-all-start.3 = ((bf16[8,64,512]{2,1,0:T(8,128)(2,1)}), bf16[8,64,512]{2,1,0:T(8,128)(2,1)}, u32[]{:S(2)}, u32[]{:S(2)}) async-start(bf16[8,64,512]{2,1,0:T(8,128)(2,1)} %convert_element_type.691), calls=%async_computation.3 | async-start | bytes 1048576 | tf_op jit(solution)/shard_map/all_to_all | solution.py:174
  140.5 3.2 %fusion = f32[512,4,128]{0,2,1:T(8,128)} fusion(f32[5,512,4]{1,0,2:T(8,128)} %copy.87, bf16[5,4,128,128]{3,2,1,0:T(8,128)(2,1)} %copy-done.25, bf16[512,4,128,1]{2,1,0,3:T(4,128)(2,1)} %bitcast.150), kind=kOutput, calls=%fused_computation.1 | convolution fusion | flops 337903616 | bytes 2269184 | tf_op jit(solution)/shard_map/phe,bhde->bphd/dot_general | solution.py:149
  143.7 2.5 %copy.100 = f32[512,4,128]{2,0,1:T(8,128)} copy(f32[512,4,128]{0,2,1:T(8,128)} %fusion) | data formatting | bytes 2097152 | tf_op jit(solution)/shard_map/reduce_sum | solution.py:147
  146.2 1.6 add_convert_fusion.2
  148.5 3.1 %collective-permute-start.8 = (bf16[2,4,128,128]{2,3,0,1:T(8,128)(2,1)}, bf16[2,4,128,128]{2,3,0,1:T(8,128)(2,1)}, u32[]{:S(2)}, u32[]{:S(2)}) collective-permute-start(bf16[2,4,128,128]{2,3,0,1:T(8,128)(2,1)} %pad_maximum_fusion.2), channel_id=1, source_target_pairs={{0,64},{64,0},{8,72},{72,8},{16,80},{80,16},{24,88},{88,24},{32,96... | collective-permute-start | bytes 786440 | tf_op jit(solution)/shard_map/ppermute | solution.py:14
  151.6 2.0 fusion.9
  154.8 2.0 convert_element_type.694
  156.8 7.3 %collective-permute-done.8 = bf16[2,4,128,128]{2,3,0,1:T(8,128)(2,1)} collective-permute-done((bf16[2,4,128,128]{2,3,0,1:T(8,128)(2,1)}, bf16[2,4,128,128]{2,3,0,1:T(8,128)(2,1)}, u32[]{:S(2)}, u32[]{:S(2)}) %collective-permute-start.8) | collective-permute-done | bytes 262176 | tf_op jit(solution)/shard_map/ppermute | solution.py:14
  164.1 1.9 add_convert_fusion.1
  166.0 1.4 collective-permute-start.9
  167.4 5.4 %all-to-all-start.5 = ((bf16[8,64,512]{2,1,0:T(8,128)(2,1)}), bf16[8,64,512]{2,1,0:T(8,128)(2,1)}, u32[]{:S(2)}, u32[]{:S(2)}) async-start(bf16[8,64,512]{2,1,0:T(8,128)(2,1)} %convert_element_type.694), calls=%async_computation.5 | async-start | bytes 1048576 | tf_op jit(solution)/shard_map/all_to_all | solution.py:175
  172.8 2.6 %convolution_bitcast_fusion = f32[512,4,128]{2,0,1:T(8,128)S(1)} fusion(bf16[4,512,512]{2,1,0:T(8,128)(2,1)} %multiply_convert_fusion.1, bf16[512,4,128]{2,1,0:T(4,128)(2,1)} %reshape.3021), kind=kOutput, calls=%fused_computation.12 | convolution fusion | flops 268435456 | bytes 3670016 | tf_op jit(solution)/shard_map/while/body/eval_jaxpr/hps,phd->shd/dot_general | solution.py:128
  175.3 1.4 collective-permute-done.9
  176.7 1.5 fusion.12
  179.4 2.0 all_to_all.107
  182.2 5.0 %all-to-all-start.6 = ((bf16[8,64,512]{2,1,0:T(8,128)(2,1)}), bf16[8,64,512]{2,1,0:T(8,128)(2,1)}, u32[]{:S(2)}, u32[]{:S(2)}) async-start(bf16[8,64,512]{2,1,0:T(8,128)(2,1)} %all_to_all.107), calls=%async_computation.6 | async-start | bytes 1048576 | tf_op jit(solution)/shard_map/all_to_all | solution.py:176
  187.7 1.4 fusion.13
  190.4 6.3 %all-to-all-done.6 = bf16[8,64,512]{2,1,0:T(8,128)(2,1)} async-done(((bf16[8,64,512]{2,1,0:T(8,128)(2,1)}), bf16[8,64,512]{2,1,0:T(8,128)(2,1)}, u32[]{:S(2)}, u32[]{:S(2)}) %all-to-all-start.6) | async-done | bytes 524320 | tf_op jit(solution)/shard_map/all_to_all | solution.py:176
  196.7 4.4 %all-to-all-start.7 = ((bf16[8,64,512]{2,1,0:T(8,128)(2,1)}), bf16[8,64,512]{2,1,0:T(8,128)(2,1)S(1)}, u32[]{:S(2)}, u32[]{:S(2)}) async-start(bf16[8,64,512]{2,1,0:T(8,128)(2,1)} %all_to_all.111), calls=%async_computation.7 | async-start | bytes 1048576 | tf_op jit(solution)/shard_map/all_to_all | solution.py:177
  201.1 1.9 copy.133
  203.0 1.9 copy.134
  204.8 1.9 copy.135
  206.7 3.7 %all-to-all-done.7 = bf16[8,64,512]{2,1,0:T(8,128)(2,1)S(1)} async-done(((bf16[8,64,512]{2,1,0:T(8,128)(2,1)}), bf16[8,64,512]{2,1,0:T(8,128)(2,1)S(1)}, u32[]{:S(2)}, u32[]{:S(2)}) %all-to-all-start.7) | async-done | bytes 524320 | tf_op jit(solution)/shard_map/all_to_all | solution.py:177
  (129 shorter events, 27.3 us)
Async XLA Ops:
  0.6 9.4 %copy-start.23 = (s32[4,15,512]{2,0,1:T(4,128)S(1)}, s32[4,15,512]{2,0,1:T(4,128)}, u32[]{:S(2)}) copy-start(s32[4,15,512]{2,0,1:T(4,128)} %param.9) | copy-start | bytes 368644
  0.6 9.5 %copy-start.9 = (bf16[64,4096]{1,0:T(8,128)(2,1)S(1)}, bf16[64,4096]{1,0:T(8,128)(2,1)}, u32[]{:S(2)}) copy-start(bf16[64,4096]{1,0:T(8,128)(2,1)} %param.8) | copy-start | bytes 1572868
  0.7 12.1 %copy-start.10 = (bf16[64,4096]{1,0:T(8,128)(2,1)S(1)}, bf16[64,4096]{1,0:T(8,128)(2,1)}, u32[]{:S(2)}) copy-start(bf16[64,4096]{1,0:T(8,128)(2,1)} %param.6) | copy-start | bytes 1572868
  2.6 16.0 %all-to-all-start.2 = ((bf16[64,8,512]{2,0,1:T(8,128)(2,1)}), bf16[64,8,512]{2,0,1:T(8,128)(2,1)S(1)}, u32[]{:S(2)}, u32[]{:S(2)}) async-start(bf16[64,8,512]{2,0,1:T(8,128)(2,1)} %bitcast.147), calls=%async_computation.2 | async-start | bytes 1048576 | tf_op jit(solution)/shard_map/all_to_all | solution.py:35
  9.2 14.4 %copy-start.11 = (bf16[64,4096]{1,0:T(8,128)(2,1)S(1)}, bf16[64,4096]{1,0:T(8,128)(2,1)}, u32[]{:S(2)}) copy-start(bf16[64,4096]{1,0:T(8,128)(2,1)} %param.5) | copy-start | bytes 1572868
  18.6 13.7 %all-to-all-start.1 = ((bf16[64,8,512]{2,0,1:T(8,128)(2,1)}), bf16[64,8,512]{2,0,1:T(8,128)(2,1)S(1)}, u32[]{:S(2)}, u32[]{:S(2)}) async-start(bf16[64,8,512]{2,0,1:T(8,128)(2,1)} %bitcast.148), calls=%async_computation.1 | async-start | bytes 1048576 | tf_op jit(solution)/shard_map/all_to_all | solution.py:34
  32.4 13.7 %all-to-all-start.4 = ((bf16[8,64,512]{2,1,0:T(8,128)(2,1)}), bf16[8,64,512]{2,1,0:T(8,128)(2,1)S(1)}, u32[]{:S(2)}, u32[]{:S(2)}) async-start(bf16[8,64,512]{2,1,0:T(8,128)(2,1)} %bitcast_dynamic-update-slice_fusion), calls=%async_computation.4 | async-start | bytes 1048576 | tf_op jit(solution)/shard_map/all_to_all | solution.py:37
  46.1 13.7 %all-to-all-start = ((bf16[64,8,512]{2,0,1:T(8,128)(2,1)}), bf16[64,8,512]{2,0,1:T(8,128)(2,1)S(1)}, u32[]{:S(2)}, u32[]{:S(2)}) async-start(bf16[64,8,512]{2,0,1:T(8,128)(2,1)} %bitcast.149), calls=%async_computation | async-start | bytes 1048576 | tf_op jit(solution)/shard_map/all_to_all | solution.py:33
  55.0 21.0 %collective-permute-start = (bf16[4,128,128]{2,1,0:T(8,128)(2,1)}, bf16[4,128,128]{2,1,0:T(8,128)(2,1)S(1)}, u32[]{:S(2)}, u32[]{:S(2)}) collective-permute-start(bf16[4,128,128]{2,1,0:T(8,128)(2,1)} %get-tuple-element.66), channel_id=1, source_target_pairs={{0,8},{8,0},{16,24},{24,16},{32,40},{40,32},{48,56},{56,48},{64,72... | collective-permute-start | bytes 393224 | tf_op jit(solution)/shard_map/ppermute | solution.py:14
  60.8 7.0 %copy-start.5 = (bf16[512,4,128]{0,2,1:T(8,128)(2,1)S(1)}, bf16[512,4,128]{0,2,1:T(8,128)(2,1)}, u32[]{:S(2)}) copy-start(bf16[512,4,128]{0,2,1:T(8,128)(2,1)} %copy.112) | copy-start | bytes 1572868
  60.8 7.0 %copy-start.12 = (pred[512,512]{1,0:T(8,128)(4,1)S(1)}, pred[512,512]{1,0:T(8,128)(4,1)}, u32[]{:S(2)}) copy-start(pred[512,512]{1,0:T(8,128)(4,1)} %iota_compare_fusion.1) | copy-start | bytes 786436
  60.8 7.0 %copy-start.13 = (pred[512,512]{1,0:T(8,128)(4,1)S(1)}, pred[512,512]{1,0:T(8,128)(4,1)}, u32[]{:S(2)}) copy-start(pred[512,512]{1,0:T(8,128)(4,1)} %get-tuple-element.56) | copy-start | bytes 786436
  60.8 7.0 %copy-start.14 = (pred[512,512]{1,0:T(8,128)(4,1)S(1)}, pred[512,512]{1,0:T(8,128)(4,1)}, u32[]{:S(2)}) copy-start(pred[512,512]{1,0:T(8,128)(4,1)} %get-tuple-element.57) | copy-start | bytes 786436
  60.8 7.0 %copy-start.15 = (pred[512,512]{1,0:T(8,128)(4,1)S(1)}, pred[512,512]{1,0:T(8,128)(4,1)}, u32[]{:S(2)}) copy-start(pred[512,512]{1,0:T(8,128)(4,1)} %get-tuple-element.58) | copy-start | bytes 786436
  60.8 7.0 %copy-start.16 = (pred[512,512]{1,0:T(8,128)(4,1)S(1)}, pred[512,512]{1,0:T(8,128)(4,1)}, u32[]{:S(2)}) copy-start(pred[512,512]{1,0:T(8,128)(4,1)} %get-tuple-element.59) | copy-start | bytes 786436
  60.8 7.0 %copy-start.17 = (pred[512,512]{1,0:T(8,128)(4,1)S(1)}, pred[512,512]{1,0:T(8,128)(4,1)}, u32[]{:S(2)}) copy-start(pred[512,512]{1,0:T(8,128)(4,1)} %get-tuple-element.60) | copy-start | bytes 786436
  60.8 7.0 %copy-start.18 = (pred[512,512]{1,0:T(8,128)(4,1)S(1)}, pred[512,512]{1,0:T(8,128)(4,1)}, u32[]{:S(2)}) copy-start(pred[512,512]{1,0:T(8,128)(4,1)} %get-tuple-element.61) | copy-start | bytes 786436
  60.8 7.0 %copy-start.19 = (pred[512,512]{1,0:T(8,128)(4,1)S(1)}, pred[512,512]{1,0:T(8,128)(4,1)}, u32[]{:S(2)}) copy-start(pred[512,512]{1,0:T(8,128)(4,1)} %get-tuple-element.62) | copy-start | bytes 786436
  60.8 7.0 %copy-start.20 = (pred[512,512]{1,0:T(8,128)(4,1)S(1)}, pred[512,512]{1,0:T(8,128)(4,1)}, u32[]{:S(2)}) copy-start(pred[512,512]{1,0:T(8,128)(4,1)} %get-tuple-element.63) | copy-start | bytes 786436
  60.8 7.0 %copy-start.21 = (pred[512,512]{1,0:T(8,128)(4,1)S(1)}, pred[512,512]{1,0:T(8,128)(4,1)}, u32[]{:S(2)}) copy-start(pred[512,512]{1,0:T(8,128)(4,1)} %get-tuple-element.64) | copy-start | bytes 786436
  60.8 7.0 %copy-start.22 = (pred[512,512]{1,0:T(8,128)(4,1)S(1)}, pred[512,512]{1,0:T(8,128)(4,1)}, u32[]{:S(2)}) copy-start(pred[512,512]{1,0:T(8,128)(4,1)} %get-tuple-element.65) | copy-start | bytes 786436
  60.9 7.0 %copy-start.26 = (f32[4,512]{1,0:T(4,128)S(1)}, f32[4,512]{1,0:T(4,128)}, u32[]{:S(2)}) copy-start(f32[4,512]{1,0:T(4,128)} %get-tuple-element.48) | copy-start | bytes 24580
  60.9 7.0 %copy-start.27 = (f32[4,512]{1,0:T(4,128)S(1)}, f32[4,512]{1,0:T(4,128)}, u32[]{:S(2)}) copy-start(f32[4,512]{1,0:T(4,128)} %get-tuple-element.49) | copy-start | bytes 24580
  60.9 7.0 %copy-start.28 = (f32[4,512]{1,0:T(4,128)S(1)}, f32[4,512]{1,0:T(4,128)}, u32[]{:S(2)}) copy-start(f32[4,512]{1,0:T(4,128)} %get-tuple-element.50) | copy-start | bytes 24580
  60.9 7.0 %copy-start.29 = (f32[4,512]{1,0:T(4,128)S(1)}, f32[4,512]{1,0:T(4,128)}, u32[]{:S(2)}) copy-start(f32[4,512]{1,0:T(4,128)} %get-tuple-element.51) | copy-start | bytes 24580
  60.9 7.0 %copy-start.30 = (f32[4,512]{1,0:T(4,128)S(1)}, f32[4,512]{1,0:T(4,128)}, u32[]{:S(2)}) copy-start(f32[4,512]{1,0:T(4,128)} %get-tuple-element.52) | copy-start | bytes 24580
  60.9 7.0 %copy-start.31 = (f32[4,512]{1,0:T(4,128)S(1)}, f32[4,512]{1,0:T(4,128)}, u32[]{:S(2)}) copy-start(f32[4,512]{1,0:T(4,128)} %get-tuple-element.53) | copy-start | bytes 24580
  60.9 7.0 %copy-start.32 = (f32[4,512]{1,0:T(4,128)S(1)}, f32[4,512]{1,0:T(4,128)}, u32[]{:S(2)}) copy-start(f32[4,512]{1,0:T(4,128)} %get-tuple-element.54) | copy-start | bytes 24580
  60.9 7.0 %copy-start.33 = (f32[4,512]{1,0:T(4,128)S(1)}, f32[4,512]{1,0:T(4,128)}, u32[]{:S(2)}) copy-start(f32[4,512]{1,0:T(4,128)} %get-tuple-element.55) | copy-start | bytes 24580
  68.0 6.6 %copy-start.7 = (bf16[512,4,128]{2,1,0:T(4,128)(2,1)S(1)}, bf16[512,4,128]{2,1,0:T(4,128)(2,1)}, u32[]{:S(2)}) copy-start(bf16[512,4,128]{2,1,0:T(4,128)(2,1)} %reshape.3021) | copy-start | bytes 1572868
  68.0 6.6 %copy-start.8 = (f32[512,4,128]{0,2,1:T(8,128)S(1)}, f32[512,4,128]{0,2,1:T(8,128)}, u32[]{:S(2)}) copy-start(f32[512,4,128]{0,2,1:T(8,128)} %copy.105) | copy-start | bytes 3145732
  68.0 6.6 %copy-start.24 = (f32[5,512,4]{1,0,2:T(8,128)S(1)}, f32[5,512,4]{1,0,2:T(8,128)}, u32[]{:S(2)}) copy-start(f32[5,512,4]{1,0,2:T(8,128)} %copy.87) | copy-start | bytes 122884
  75.4 37.1 %copy-start.1 = (f32[5,4,128,128]{2,3,0,1:T(8,128)}, f32[5,4,128,128]{2,3,0,1:T(8,128)S(1)}, u32[]{:S(2)}) copy-start(f32[5,4,128,128]{2,3,0,1:T(8,128)S(1)} %get-tuple-element.69) | copy-start | bytes 3932164
  75.4 36.9 %collective-permute-start.5 = (bf16[5,4,128,128]{2,3,0,1:T(8,128)(2,1)S(1)}, bf16[5,4,128,128]{2,3,0,1:T(8,128)(2,1)S(1)}, u32[]{:S(2)}, u32[]{:S(2)}) collective-permute-start(bf16[5,4,128,128]{2,3,0,1:T(8,128)(2,1)S(1)} %get-tuple-element.68), channel_id=1, source_target_pairs={{0,8},{8,0},{16,24},{24,16},{32,40},{40,32},{48,56},{56,48},{64,72... | collective-permute-start | bytes 1966088 | tf_op jit(solution)/shard_map/ppermute | solution.py:14
  76.0 18.9 %collective-permute-start.1 = (bf16[4,128,128]{2,1,0:T(8,128)(2,1)S(1)}, bf16[4,128,128]{2,1,0:T(8,128)(2,1)S(1)}, u32[]{:S(2)}, u32[]{:S(2)}) collective-permute-start(bf16[4,128,128]{2,1,0:T(8,128)(2,1)S(1)} %fusion.38), channel_id=1, source_target_pairs={{0,16},{16,0},{8,24},{24,8},{32,48},{48,32},{40,56},{56,40},{64,80... | collective-permute-start | bytes 393224 | tf_op jit(solution)/shard_map/ppermute | solution.py:14
  95.0 4.1 %collective-permute-start.2 = (bf16[4,128,128]{2,1,0:T(8,128)(2,1)S(1)}, bf16[4,128,128]{2,1,0:T(8,128)(2,1)S(1)}, u32[]{:S(2)}, u32[]{:S(2)}) collective-permute-start(bf16[4,128,128]{2,1,0:T(8,128)(2,1)S(1)} %fusion.85), channel_id=1, source_target_pairs={{0,32},{32,0},{8,40},{40,8},{16,48},{48,16},{24,56},{56,24},{64,96... | collective-permute-start | bytes 393224 | tf_op jit(solution)/shard_map/ppermute | solution.py:14
  99.2 6.8 %collective-permute-start.3 = (bf16[4,128,128]{2,1,0:T(8,128)(2,1)S(1)}, bf16[4,128,128]{2,1,0:T(8,128)(2,1)S(1)}, u32[]{:S(2)}, u32[]{:S(2)}) collective-permute-start(bf16[4,128,128]{2,1,0:T(8,128)(2,1)S(1)} %fusion.39), channel_id=1, source_target_pairs={{0,64},{64,0},{8,72},{72,8},{16,80},{80,16},{24,88},{88,24},{32,96... | collective-permute-start | bytes 393224 | tf_op jit(solution)/shard_map/ppermute | solution.py:14
  106.1 8.7 %collective-permute-start.4 = (bf16[4,128,128]{2,1,0:T(8,128)(2,1)S(1)}, bf16[4,128,128]{2,1,0:T(8,128)(2,1)S(1)}, u32[]{:S(2)}, u32[]{:S(2)}) collective-permute-start(bf16[4,128,128]{2,1,0:T(8,128)(2,1)S(1)} %fusion.34), channel_id=1, source_target_pairs={{0,128},{128,0},{8,136},{136,8},{16,144},{144,16},{24,152},{152,24... | collective-permute-start | bytes 393224 | tf_op jit(solution)/shard_map/ppermute | solution.py:14
  114.0 10.6 %collective-permute-start.6 = (bf16[4,4,128,128]{2,3,0,1:T(8,128)(2,1)}, bf16[4,4,128,128]{2,3,0,1:T(8,128)(2,1)}, u32[]{:S(2)}, u32[]{:S(2)}) collective-permute-start(bf16[4,4,128,128]{2,3,0,1:T(8,128)(2,1)} %pad_maximum_fusion), channel_id=1, source_target_pairs={{0,16},{16,0},{8,24},{24,8},{32,48},{48,32},{40,56},{56,40},{64,80... | collective-permute-start | bytes 1572872 | tf_op jit(solution)/shard_map/ppermute | solution.py:14
  120.1 6.8 %copy-start.3 = (f32[512,4,128]{2,0,1:T(8,128)S(1)}, f32[512,4,128]{2,0,1:T(8,128)}, u32[]{:S(2)}) copy-start(f32[512,4,128]{2,0,1:T(8,128)} %copy.92) | copy-start | bytes 3145732
  126.9 19.3 %collective-permute-start.7 = (bf16[3,4,128,128]{2,3,0,1:T(8,128)(2,1)}, bf16[3,4,128,128]{2,3,0,1:T(8,128)(2,1)S(1)}, u32[]{:S(2)}, u32[]{:S(2)}) collective-permute-start(bf16[3,4,128,128]{2,3,0,1:T(8,128)(2,1)} %pad_maximum_fusion.1), channel_id=1, source_target_pairs={{0,32},{32,0},{8,40},{40,8},{16,48},{48,16},{24,56},{56,24},{64,96... | collective-permute-start | bytes 1179656 | tf_op jit(solution)/shard_map/ppermute | solution.py:14
  130.9 36.5 %all-to-all-start.3 = ((bf16[8,64,512]{2,1,0:T(8,128)(2,1)}), bf16[8,64,512]{2,1,0:T(8,128)(2,1)}, u32[]{:S(2)}, u32[]{:S(2)}) async-start(bf16[8,64,512]{2,1,0:T(8,128)(2,1)} %convert_element_type.691), calls=%async_computation.3 | async-start | bytes 1048576 | tf_op jit(solution)/shard_map/all_to_all | solution.py:174
  148.5 15.6 %collective-permute-start.8 = (bf16[2,4,128,128]{2,3,0,1:T(8,128)(2,1)}, bf16[2,4,128,128]{2,3,0,1:T(8,128)(2,1)}, u32[]{:S(2)}, u32[]{:S(2)}) collective-permute-start(bf16[2,4,128,128]{2,3,0,1:T(8,128)(2,1)} %pad_maximum_fusion.2), channel_id=1, source_target_pairs={{0,64},{64,0},{8,72},{72,8},{16,80},{80,16},{24,88},{88,24},{32,96... | collective-permute-start | bytes 786440 | tf_op jit(solution)/shard_map/ppermute | solution.py:14
  166.0 10.7 %collective-permute-start.9 = (bf16[1,4,128,128]{2,3,0,1:T(8,128)(2,1)}, bf16[1,4,128,128]{2,3,0,1:T(8,128)(2,1)}, u32[]{:S(2)}, u32[]{:S(2)}) collective-permute-start(bf16[1,4,128,128]{2,3,0,1:T(8,128)(2,1)} %add_convert_fusion.1), channel_id=1, source_target_pairs={{0,128},{128,0},{8,136},{136,8},{16,144},{144,16},{24,152},{152,24... | collective-permute-start | bytes 393224 | tf_op jit(solution)/shard_map/ppermute | solution.py:14
  167.4 14.9 %all-to-all-start.5 = ((bf16[8,64,512]{2,1,0:T(8,128)(2,1)}), bf16[8,64,512]{2,1,0:T(8,128)(2,1)}, u32[]{:S(2)}, u32[]{:S(2)}) async-start(bf16[8,64,512]{2,1,0:T(8,128)(2,1)} %convert_element_type.694), calls=%async_computation.5 | async-start | bytes 1048576 | tf_op jit(solution)/shard_map/all_to_all | solution.py:175
  178.2 9.1 %copy-start.6 = (bf16[512,4,128]{0,2,1:T(8,128)(2,1)S(1)}, bf16[512,4,128]{0,2,1:T(8,128)(2,1)}, u32[]{:S(2)}) copy-start(bf16[512,4,128]{0,2,1:T(8,128)(2,1)} %copy.112) | copy-start | bytes 1572868
  182.2 14.5 %all-to-all-start.6 = ((bf16[8,64,512]{2,1,0:T(8,128)(2,1)}), bf16[8,64,512]{2,1,0:T(8,128)(2,1)}, u32[]{:S(2)}, u32[]{:S(2)}) async-start(bf16[8,64,512]{2,1,0:T(8,128)(2,1)} %all_to_all.107), calls=%async_computation.6 | async-start | bytes 1048576 | tf_op jit(solution)/shard_map/all_to_all | solution.py:176
  196.7 13.7 %all-to-all-start.7 = ((bf16[8,64,512]{2,1,0:T(8,128)(2,1)}), bf16[8,64,512]{2,1,0:T(8,128)(2,1)S(1)}, u32[]{:S(2)}, u32[]{:S(2)}) async-start(bf16[8,64,512]{2,1,0:T(8,128)(2,1)} %all_to_all.111), calls=%async_computation.7 | async-start | bytes 1048576 | tf_op jit(solution)/shard_map/all_to_all | solution.py:177
  (4 other events, 9.7 us)
